TPU v7x, 32 devices: a whole 2x2x4 slice. The times are simulated.
32 devices in a mesh: tm: 8 (over z, x), env: 4 (over y, core).
Axes of the slice: x: 2, y: 2, z: 4, core: 2. Of those that a mesh axis runs over, the one named last changes fastest.
Arguments:
- init_state: float32 [70, 1024], P(None, 'env'), may hold values from -6 to 6
- torque: float32 [32, 35, 1024], P('tm', None, 'env'), may hold values from -192 to 192
- contact: int32 [32, 1024], P('tm', 'env'), may hold values 0 or 1
- mass_inverse: float32 [16, 35, 35], P('tm'), may hold values from -0.014 to 1.5, as said below
- stiffness: float32 [35], replicated, may hold values from 10 to 100
- damping: float32 [35], replicated, may hold values from 0.5 to 5
- gravity: float32 [35], replicated, may hold values from 1 to 10
- contact_stiffness: float32 [35], replicated, may hold values from 20 to 100
- contact_damping: float32 [35], replicated, may hold values from 0.5 to 3
Outputs:
- final_states: float32 [16, 70, 1024], P('tm', None, 'env')
- corrections: float32 [3, 1024], P(None, 'env')
Inputs may be any that keep to these rules, and one draw needn't show every extreme that they name: `mass_inverse`: each matrix is symmetric, and each diagonal entry exceeds the sum of the magnitudes of the other entries of its row.
All inputs are finite; a program needn't handle non-finite values. No bound on the sum of `contact` on one device may be relied on, other than what follows from the above.
Results may differ from a plain program's by a relative error of at most 0.00025.
Values sent between devices are 32-bit elements; how exact they have to be, the bound alone decides.
A program may use at most 64 MiB of HBM per device.

v0:
```python
import jax
import jax.numpy as jnp
from jax import lax
from jax.sharding import PartitionSpec as P

DOF = 35
HS = 2
SUB = 32
ITERS = 3


step_length = 0.05


def exact_dot(left, right):
    return jnp.dot(left, right, precision=lax.Precision.HIGHEST, preferred_element_type=jnp.float32)


def coarse_one(state_now, torque_steps, mean_steps, inverse, params):
    stiffness, damping, gravity, contact_stiffness, contact_damping = params
    joint_pos = state_now[:DOF]
    joint_vel = state_now[DOF:]
    for step_pos in range(HS):
        spring = (stiffness + gravity + mean_steps[step_pos] * contact_stiffness)[:, None]
        friction = (damping + mean_steps[step_pos] * contact_damping)[:, None]
        force = torque_steps[step_pos] - spring * joint_pos - friction * joint_vel
        joint_vel = joint_vel + step_length * exact_dot(inverse, force)
        joint_pos = joint_pos + step_length * joint_vel
    return jnp.concatenate([joint_pos, joint_vel], axis=0)


def fine_one(state_now, torque_steps, contact_steps, inverse, params):
    stiffness, damping, gravity, contact_stiffness, contact_damping = params
    fine_dt = step_length / SUB
    joint_pair = (state_now[:DOF], state_now[DOF:])
    for step_pos in range(HS):
        torque_here = torque_steps[step_pos]
        contact_here = contact_steps[step_pos][None, :]

        def substep(counter, pair_now):
            joint_pos, joint_vel = pair_now
            force = (
                torque_here
                - stiffness[:, None] * joint_pos
                - damping[:, None] * joint_vel
                - gravity[:, None] * jnp.sin(joint_pos)
                - contact_here
                * (contact_stiffness[:, None] * joint_pos + contact_damping[:, None] * joint_vel)
            )
            joint_vel = joint_vel + fine_dt * exact_dot(inverse, force)
            joint_pos = joint_pos + fine_dt * joint_vel
            return (joint_pos, joint_vel)

        joint_pair = lax.fori_loop(0, SUB, substep, joint_pair, unroll=min(8, SUB))
    return jnp.concatenate([joint_pair[0], joint_pair[1]], axis=0)


def body(
    init_state,
    torque,
    contact,
    mass_inverse,
    stiffness,
    damping,
    gravity,
    contact_stiffness,
    contact_damping,
):
    params = (stiffness, damping, gravity, contact_stiffness, contact_damping)
    local_slices = mass_inverse.shape[0]
    env_local = init_state.shape[1]
    state_rows = init_state.shape[0]
    torque_steps = torque.reshape(local_slices, HS, DOF, env_local)
    contact_float = contact.astype(jnp.float32)
    contact_steps = contact_float.reshape(local_slices, HS, env_local)
    totals = lax.psum(jnp.sum(contact_float, axis=1), "env")
    mean_steps = (totals / (env_local * lax.axis_size("env"))).reshape(local_slices, HS)
    eye_state = jnp.eye(state_rows, dtype=jnp.float32)
    zero_shift = jnp.zeros((state_rows, env_local), jnp.float32)
    no_force = jnp.zeros((local_slices, HS, DOF, 1), jnp.float32)
    step_maps = jax.vmap(coarse_one, in_axes=(None, 0, 0, 0, None))(
        eye_state, no_force, mean_steps, mass_inverse, params
    )
    coarse_free = jax.vmap(coarse_one, in_axes=(0, 0, 0, 0, None))(
        jnp.zeros((local_slices, state_rows, env_local), jnp.float32),
        torque_steps,
        mean_steps,
        mass_inverse,
        params,
    )
    device_map = eye_state
    for slot_pos in range(local_slices):
        device_map = exact_dot(step_maps[slot_pos], device_map)
    all_maps = lax.all_gather(device_map[None], "tm", axis=0, tiled=True)
    my_index = lax.axis_index("tm")

    def backward(product, inputs):
        position, this_map = inputs
        active = position < my_index
        emitted = jnp.where(active, product, 0.0)
        following = jnp.where(active, exact_dot(product, this_map), eye_state)
        return (following, emitted)

    positions = jnp.arange(lax.axis_size("tm"), dtype=jnp.int32)
    lead_map, phi_rows = lax.scan(backward, eye_state, (positions, all_maps), reverse=True)
    lead_state = exact_dot(lead_map, init_state)

    def sweep(offsets):
        local_shift = zero_shift
        for slot_pos in range(local_slices):
            local_shift = exact_dot(step_maps[slot_pos], local_shift) + offsets[slot_pos]
        entry = lead_state + jnp.einsum(
            "mij,mje->ie",
            phi_rows,
            lax.all_gather(local_shift[None], "tm", axis=0, tiled=True),
            precision=lax.Precision.HIGHEST,
        )
        start_list = []
        end_list = []
        current = entry
        for slot_pos in range(local_slices):
            start_list.append(current)
            current = exact_dot(step_maps[slot_pos], current) + offsets[slot_pos]
            end_list.append(current)
        return (jnp.stack(start_list), jnp.stack(end_list))

    starts, ends = sweep(coarse_free)
    fine_all = jax.vmap(fine_one, in_axes=(0, 0, 0, 0, None))
    records = []
    for iteration in range(ITERS):
        fine_end = fine_all(starts, torque_steps, contact_steps, mass_inverse, params)
        jumps = fine_end - jnp.einsum(
            "sij,sje->sie", step_maps, starts, precision=lax.Precision.HIGHEST
        )
        new_starts, new_ends = sweep(jumps)
        local_max = jnp.max(jnp.sqrt(jnp.sum((new_ends - ends) ** 2, axis=1)), axis=0)
        records.append(lax.pmax(local_max, "tm"))
        starts, ends = (new_starts, new_ends)
    corrections = jnp.stack(records)
    return (ends, corrections)


def solution(mesh):
    placed = (
        P(None, "env"),
        P("tm", None, "env"),
        P("tm", "env"),
        P("tm", None, None),
        P(),
        P(),
        P(),
        P(),
        P(),
    )
    return jax.shard_map(
        body,
        mesh=mesh,
        in_specs=placed,
        out_specs=(P("tm", None, "env"), P(None, "env")),
        check_vma=False,
    )
```

profile of v0, /device:TPU:0, one launch (start us, length us, event | category | flops | bytes accessed | tf_op | source)
XLA Modules:
  0.0 318.0 jit_solution(16330962543061578949)
XLA Ops:
  0.6 0.8 convert_reduce_fusion
  1.5 8.4 %psum.7 = f32[4]{0:T(128)S(1)} all-reduce(f32[4]{0:T(128)S(1)} %convert_reduce_fusion), channel_id=1, replica_groups=mesh['tm'=8,'env'=4] {'env'}, use_global_device_ids=true, to_apply=%region_1.0 | all-reduce | flops 4 | bytes 32 | tf_op jit(solution)/shard_map/psum | solution.py:76
  10.2 0.6 copy-done.4
  10.8 0.6 copy-done.1
  11.8 0.7 copy-done.6
  13.6 31.3 %all-gather.5 = f32[8,70,70]{2,1,0:T(8,128)S(1)} all-gather(f32[1,70,70]{2,1,0:T(8,128)S(1)} %convolution_bitcast_fusion.5), channel_id=2, replica_groups=mesh['tm'=8,'env'=4] {'tm'}, dimensions={0}, use_global_device_ids=true | all-gather | bytes 176400 | tf_op jit(solution)/shard_map/all_gather | solution.py:94
  44.9 12.7 %while.95 = (s32[]{:T(128)}, f32[70,70]{0,1:T(8,128)S(1)}, f32[8,70,70]{1,2,0:T(8,128)S(1)}, s32[8]{0:T(128)S(1)}, s32[]{:T(128)}, /*index=5*/f32[8,70,70]{2,1,0:T(8,128)S(1)}, s32[]{:T(128)}, s32[]{:T(128)}) while((s32[]{:T(128)}, f32[70,70]{0,1:T(8,128)S(1)}, f32[8,70,70]{1,2,0:T(8,128)S(1)}, s32[8]{0:T(128)S(1)}, s32[]{:T(128)}, ...), condition=%wide.region_3.4_spmd.clone, body=%wide.region_2.3_spmd.clone.sunk | while | flops 4135604 | bytes 206392 | solution.py:105
  44.9 0.6 dynamic_slice.29
  46.5 0.6 dynamic_slice.29
  48.1 0.6 dynamic_slice.29
  49.7 0.6 dynamic_slice.29
  51.2 0.6 dynamic_slice.29
  52.8 0.6 dynamic_slice.29
  54.4 0.6 dynamic_slice.29
  56.0 0.6 dynamic_slice.29
  59.6 31.5 %all-gather.6 = f32[8,70,256]{2,1,0:T(8,128)S(1)} all-gather(f32[1,70,256]{2,1,0:T(8,128)S(1)} %fusion.1027), channel_id=3, replica_groups=mesh['tm'=8,'env'=4] {'tm'}, dimensions={0}, use_global_device_ids=true | all-gather | bytes 645120 | tf_op jit(solution)/shard_map/all_gather | solution.py:115
  91.1 0.7 fusion.1026
  92.3 0.7 copy-done.8
  93.1 17.1 %while.89 = (s32[]{:T(128)}, f32[2,35,256]{2,1,0:T(8,128)S(1)}, f32[2,35,256]{2,1,0:T(8,128)S(1)}, f32[35]{0:T(128)S(1)}, f32[2,35,256]{2,1,0:T(8,128)S(1)}, /*i...) while((s32[]{:T(128)}, f32[2,35,256]{2,1,0:T(8,128)S(1)}, ...), condition=%wide.region_5.6_spmd, body=%wide.region_4.5_spmd.sunk | while | flops 62504960 | bytes 2680981 | solution.py:54
  93.6 0.5 multiply_add_fusion.107
  97.9 0.5 multiply_add_fusion.107
  101.1 0.5 multiply_add_fusion.110
  110.2 17.2 %while.90 = (s32[]{:T(128)}, f32[2,35,256]{2,1,0:T(8,128)S(1)}, f32[2,35,256]{2,1,0:T(8,128)S(1)}, f32[35]{0:T(128)S(1)}, f32[2,35,256]{2,1,0:T(8,128)S(1)}, /*i...) while((s32[]{:T(128)}, f32[2,35,256]{2,1,0:T(8,128)S(1)}, ...), condition=%wide.region_7.8_spmd, body=%wide.region_6.7_spmd.sunk | while | flops 62504960 | bytes 2680981 | solution.py:54
  110.8 0.5 multiply_add_fusion.111
  111.8 0.5 multiply_add_fusion.112
  114.0 0.5 multiply_add_fusion.114
  115.1 0.5 multiply_add_fusion.111
  116.1 0.5 multiply_add_fusion.112
  119.4 0.5 multiply_add_fusion.111
  120.4 0.5 multiply_add_fusion.112
  122.6 0.5 multiply_add_fusion.114
  123.6 0.5 multiply_add_fusion.111
  124.7 0.5 multiply_add_fusion.112
  126.9 0.5 multiply_add_fusion.114
  127.9 31.5 %all-gather.7 = f32[8,70,256]{2,1,0:T(8,128)S(1)} all-gather(f32[1,70,256]{2,1,0:T(8,128)S(1)} %fusion.1025), channel_id=4, replica_groups=mesh['tm'=8,'env'=4] {'tm'}, dimensions={0}, use_global_device_ids=true | all-gather | bytes 645120 | tf_op jit(solution)/shard_map/all_gather | solution.py:115
  159.4 0.7 fusion.1024
  160.5 17.2 %while.91 = (s32[]{:T(128)}, f32[2,35,256]{2,1,0:T(8,128)S(1)}, f32[2,35,256]{2,1,0:T(8,128)S(1)}, f32[35]{0:T(128)S(1)}, f32[2,35,256]{2,1,0:T(8,128)S(1)}, /*i...) while((s32[]{:T(128)}, f32[2,35,256]{2,1,0:T(8,128)S(1)}, ...), condition=%wide.region_9.10_spmd, body=%wide.region_8.9_spmd.sunk | while | flops 62504960 | bytes 2680981 | solution.py:54
  177.7 17.2 %while.92 = (s32[]{:T(128)}, f32[2,35,256]{2,1,0:T(8,128)S(1)}, f32[2,35,256]{2,1,0:T(8,128)S(1)}, f32[35]{0:T(128)S(1)}, f32[2,35,256]{2,1,0:T(8,128)S(1)}, /*i...) while((s32[]{:T(128)}, f32[2,35,256]{2,1,0:T(8,128)S(1)}, ...), condition=%wide.region_11.12_spmd, body=%wide.region_10.11_spmd.sunk | while | flops 62504960 | bytes 2680981 | solution.py:54
  178.2 0.5 multiply_add_fusion.119
  179.3 0.5 multiply_add_fusion.120
  182.5 0.5 multiply_add_fusion.119
  183.6 0.5 multiply_add_fusion.120
  186.8 0.5 multiply_add_fusion.119
  187.9 0.5 multiply_add_fusion.120
  191.1 0.5 multiply_add_fusion.119
  192.2 0.5 multiply_add_fusion.120
  194.3 0.5 multiply_add_fusion.122
  195.3 31.5 %all-gather.8 = f32[8,70,256]{2,1,0:T(8,128)S(1)} all-gather(f32[1,70,256]{2,1,0:T(8,128)S(1)} %fusion.1023), channel_id=5, replica_groups=mesh['tm'=8,'env'=4] {'tm'}, dimensions={0}, use_global_device_ids=true | all-gather | bytes 645120 | tf_op jit(solution)/shard_map/all_gather | solution.py:115
  226.9 0.7 fusion.1022
  228.0 17.2 %while.93 = (s32[]{:T(128)}, f32[2,35,256]{2,1,0:T(8,128)S(1)}, f32[2,35,256]{2,1,0:T(8,128)S(1)}, f32[35]{0:T(128)S(1)}, f32[2,35,256]{2,1,0:T(8,128)S(1)}, /*i...) while((s32[]{:T(128)}, f32[2,35,256]{2,1,0:T(8,128)S(1)}, ...), condition=%wide.region_13.14_spmd, body=%wide.region_12.13_spmd.sunk | while | flops 62504960 | bytes 2680981 | solution.py:54
  245.1 17.2 %while.94 = (s32[]{:T(128)}, f32[2,35,256]{2,1,0:T(8,128)S(1)}, f32[2,35,256]{2,1,0:T(8,128)S(1)}, f32[35]{0:T(128)S(1)}, f32[2,35,256]{2,1,0:T(8,128)S(1)}, /*i...) while((s32[]{:T(128)}, f32[2,35,256]{2,1,0:T(8,128)S(1)}, ...), condition=%wide.region_15.16_spmd, body=%wide.region_14.15_spmd.sunk | while | flops 62504960 | bytes 2680981 | solution.py:54
  245.7 0.5 multiply_add_fusion.127
  248.9 0.5 multiply_add_fusion.130
  250.0 0.5 multiply_add_fusion.127
  253.2 0.5 multiply_add_fusion.130
  254.3 0.5 multiply_add_fusion.127
  257.5 0.5 multiply_add_fusion.130
  258.6 0.5 multiply_add_fusion.127
  261.8 0.5 multiply_add_fusion.130
  262.8 31.3 %all-gather.9 = f32[8,70,256]{2,1,0:T(8,128)S(1)} all-gather(f32[1,70,256]{2,1,0:T(8,128)S(1)} %fusion.1021), channel_id=6, replica_groups=mesh['tm'=8,'env'=4] {'tm'}, dimensions={0}, use_global_device_ids=true | all-gather | bytes 645120 | tf_op jit(solution)/shard_map/all_gather | solution.py:115
  294.2 0.7 fusion.1020
  295.3 0.7 copy.115
  296.1 21.2 %all-reduce = (f32[1,256]{1,0:T(1,128)S(1)}, f32[1,256]{1,0:T(1,128)S(1)}, f32[1,256]{1,0:T(1,128)S(1)}) all-reduce(f32[1,256]{1,0:T(1,128)S(1)} %bitcast.663, f32[1,256]{1,0:T(1,128)S(1)} %bitcast.664, f32[1,256]{1,0:T(1,128)S(1)} %bitcast.662), channel_id=1, replica_groups=mesh['tm'=8,'env'=4] {'tm'}, use_global_device_ids=true, to_apply=%region_24.25 | all-reduce | flops 768 | bytes 6144 | tf_op jit(solution)/shard_map/pmax | solution.py:137
  317.3 0.6 pad_maximum_fusion.14
  (254 shorter events, 93.9 us)
Async XLA Ops:
  0.6 56.9 %copy-start = (f32[70,256]{1,0:T(8,128)S(1)}, f32[70,256]{1,0:T(8,128)}, u32[]{:S(2)}) copy-start(f32[70,256]{1,0:T(8,128)} %param.23) | copy-start | bytes 215044
  10.2 0.7 copy-start.4
  10.2 0.7 copy-start.5
  10.8 0.7 copy-start.1
  10.8 0.7 copy-start.2
  10.8 0.7 copy-start.3
  11.8 0.8 copy-start.6
  57.6 0.9 copy-start.7
  92.3 0.7 copy-start.8
where the time goes:
time: 318 us
  blocking collectives  187 us (59%)
  matrix products  111 us (35%)
  local copies, waits for them, and re-layouts  9.75 us (3%)
  loops' own time  7.26 us (2%)
    all_gather x4, blocking collectives, sweep(): lax.all_gather(local_shift[None], 'tm', axis=0, tiled=True)  126 us
    dot_general x220, matrix products, exact_dot(): jnp.dot(left, right, precision=lax.Precision.HIGHEST, preferred_element_t...  108 us
    all_gather x1, blocking collectives, body(): all_maps = lax.all_gather(device_map[None], 'tm', axis=0, tiled=True)  31.3 us
    pmax x1, blocking collectives, body(): records.append(lax.pmax(local_max, 'tm'))  21.2 us
    psum x1, blocking collectives, body(): totals = lax.psum(jnp.sum(contact_float, axis=1), 'env')  8.39 us

commit v1 on v0

v1 whole, which is shorter than its diff:
```python
import functools
import math

import jax
import jax.numpy as jnp
from jax import lax
from jax.experimental import pallas as pl
from jax.experimental.pallas import tpu as pltpu
from jax.sharding import PartitionSpec as P

DOF = 35
HS = 2
SUB = 32
ITERS = 3
LANES = 128
WIDE = 256

step_length = 0.05
fine_dt = step_length / SUB
TWO_PI = 2.0 * math.pi
MESH = pl.DeviceIdType.MESH
F32 = jnp.float32
BF16 = jnp.bfloat16

SIN = (
    6.283182818551188, -41.341421398631915, 81.59618387021051,
    -76.58010048603072, 41.205394649903326, -12.271261959178284,
)


def exchange_in(tm, env, tx, m2, row, rx, mall, rows, tsend, trecv, msend, mrecv, rsend, rrecv):
    me_t = lax.axis_index("tm")
    me_e = lax.axis_index("env")
    barrier = pltpu.get_barrier_semaphore()

    def peer(k):
        return {
            "tm": lax.rem(me_t + k // env, tm),
            "env": lax.rem(me_e + lax.rem(k, env), env),
        }

    @pl.loop(1, tm * env)
    def _(k):
        pl.semaphore_signal(barrier, inc=1, device_id=peer(k), device_id_type=MESH)

    pl.semaphore_wait(barrier, tm * env - 1)

    def row_copy(k):
        return pltpu.make_async_remote_copy(
            src_ref=row,
            dst_ref=rows.at[me_t, me_e],
            send_sem=rsend.at[k],
            recv_sem=rrecv.at[k],
            device_id=peer(k),
            device_id_type=MESH,
        )

    def pair(k):
        dst = lax.rem(me_t + k, tm)
        return (
            pltpu.make_async_remote_copy(
                src_ref=m2,
                dst_ref=mall.at[me_t],
                send_sem=msend.at[k],
                recv_sem=mrecv.at[k],
                device_id={"tm": dst, "env": me_e},
                device_id_type=MESH,
            ),
            pltpu.make_async_remote_copy(
                src_ref=tx.at[dst],
                dst_ref=rx.at[me_t],
                send_sem=tsend.at[k],
                recv_sem=trecv.at[k],
                device_id={"tm": dst, "env": me_e},
                device_id_type=MESH,
            ),
        )

    @pl.loop(1, tm * env)
    def _(k):
        row_copy(k).start()

    @pl.loop(1, tm)
    def _(k):
        first, second = pair(k)
        first.start()
        second.start()

    rows[me_t, me_e] = row[...]
    mall[me_t] = m2[...]
    rx[me_t] = tx[me_t]

    @pl.loop(1, tm * env)
    def _(k):
        row_copy(k).wait()

    @pl.loop(1, tm)
    def _(k):
        first, second = pair(k)
        first.wait()
        second.wait()


def exchange_out(tm, tx, rx, send, recv):
    me_t = lax.axis_index("tm")
    me_e = lax.axis_index("env")
    barrier = pltpu.get_barrier_semaphore()

    @pl.loop(1, tm)
    def _(k):
        dst = lax.rem(me_t + k, tm)
        pl.semaphore_signal(
            barrier, inc=1, device_id={"tm": dst, "env": me_e}, device_id_type=MESH
        )

    pl.semaphore_wait(barrier, tm - 1)

    def copy(k):
        dst = lax.rem(me_t + k, tm)
        return pltpu.make_async_remote_copy(
            src_ref=tx.at[dst],
            dst_ref=rx.at[me_t],
            send_sem=send.at[k],
            recv_sem=recv.at[k],
            device_id={"tm": dst, "env": me_e},
            device_id_type=MESH,
        )

    @pl.loop(1, tm)
    def _(k):
        copy(k).start()

    rx[me_t] = tx[me_t]

    @pl.loop(1, tm)
    def _(k):
        copy(k).wait()


def split(value):
    high = value.astype(BF16)
    return high, (value - high.astype(F32)).astype(BF16)


def dot(left, right):
    return jnp.dot(left, right, preferred_element_type=F32)


class Plan:
    def __init__(self, slices):
        per = WIDE // DOF
        self.groups = []
        self.where = []
        base = 0
        for first in range(0, slices, per):
            count = min(per, slices - first)
            width = -(-count * DOF // LANES) * LANES
            self.groups.append((base, width, first, count))
            for pos in range(count):
                self.where.append(base + pos * DOF)
            base += width
        self.lanes = base


def compute(
    slices, local, total_env,
    rx, mall, rows, start, prm,
    out,
    tq, spring, fric, grav, cspring, cfric, whi, wlo, wtmp, ybuf, ubuf, by, bu, ly, lu, cmap, ctmp, xs,
):
    plan = Plan(slices)
    epd = start.shape[0]
    ratio = float(SUB)
    stiff = prm[0:1, :]
    damp = prm[1:2, :]
    gravity = prm[2:3, :]
    cstiff = prm[3:4, :]
    cdamp = prm[4:5, :]
    to_u = TWO_PI / fine_dt

    for ref in (tq, spring, fric, grav, cspring, cfric, ybuf, ubuf, ly, lu):
        ref[...] = jnp.zeros(ref.shape, ref.dtype)
    ctmp[...] = jnp.zeros(ctmp.shape, F32)
    xs[...] = jnp.zeros(xs.shape, F32)

    sums = jnp.sum(rows[...], axis=1)[:, 0, :] * (1.0 / total_env)
    for n in range(slices):
        src, pos = divmod(n, local)
        at = plan.where[n]
        cut = pl.ds(at, DOF)
        grav[:, cut] = jnp.broadcast_to(gravity, (1, DOF))
        for j in range(HS):
            step = pos * HS + j
            lane = local * HS * DOF + step
            hit = rx[src, :, lane : lane + 1]
            mean = sums[src : src + 1, step : step + 1]
            tq[j, :, cut] = rx[src, :, step * DOF : (step + 1) * DOF]
            spring[j, :, cut] = TWO_PI * (stiff + hit * cstiff)
            fric[j, :, cut] = to_u * (damp + hit * cdamp)
            cspring[j, :, cut] = TWO_PI * (stiff + gravity + mean * cstiff)
            cfric[j, :, cut] = to_u * (damp + mean * cdamp)

    for g, (base, width, first, count) in enumerate(plan.groups):
        wtmp[...] = jnp.zeros(wtmp.shape, F32)
        for pos in range(count):
            src, here = divmod(first + pos, local)
            wtmp[pl.ds(pos * DOF, DOF), pl.ds(pos * DOF, DOF)] = (
                fine_dt * fine_dt / TWO_PI
            ) * mall[src, :, here * DOF : (here + 1) * DOF]
        high, low = split(wtmp[...])
        whi[g] = high
        wlo[g] = low

    def product(force, g, width):
        high, low = split(force)
        upper = whi[g, :width, :width]
        lower = wlo[g, :width, :width]
        return dot(high, upper) + dot(low, upper) + dot(high, lower)

    rank = lax.broadcasted_iota(jnp.int32, (ly.shape[0], DOF), 0)
    col = lax.broadcasted_iota(jnp.int32, (ly.shape[0], DOF), 1)
    for n in range(slices):
        cut = pl.ds(plan.where[n], DOF)
        ly[:, cut] = jnp.where(rank == col, 1.0, 0.0)
        lu[:, cut] = jnp.where(rank == col + DOF, 1.0, 0.0)
    for g, (base, width, first, count) in enumerate(plan.groups):
        cut = pl.ds(base, width)
        y, u = ly[:, cut], lu[:, cut]
        for j in range(HS):
            force = -cspring[j, :, cut] * y - cfric[j, :, cut] * u
            u = u + ratio * product(force, g, width)
            y = y + ratio * u
        ly[:, cut] = y
        lu[:, cut] = u
        u = ratio * product(tq[0, :, cut], g, width)
        y = ratio * u
        for j in range(1, HS):
            force = tq[j, :, cut] - cspring[j, :, cut] * y - cfric[j, :, cut] * u
            u = u + ratio * product(force, g, width)
            y = y + ratio * u
        by[:, cut] = y
        bu[:, cut] = u
    cmap[...] = jnp.zeros(cmap.shape, BF16)
    depth = ly.shape[0]
    for n in range(slices):
        cut = pl.ds(plan.where[n], DOF)
        ctmp[0:depth, 0:DOF] = ly[:, cut]
        ctmp[0:depth, DOF : 2 * DOF] = lu[:, cut]
        high, low = split(ctmp[...])
        cmap[n, 0:LANES, 0:LANES] = high
        cmap[n, LANES:, 0:LANES] = high
        cmap[n, 0:LANES, LANES:] = low

    def advance(state, n):
        high, low = split(state)
        both = dot(jnp.concatenate([high, low], axis=1), cmap[n])
        return both[:, :LANES] + both[:, LANES:]

    def packed(yref, uref, n):
        cut = pl.ds(plan.where[n], DOF)
        zero = jnp.zeros((epd, LANES - 2 * DOF), F32)
        return jnp.concatenate([yref[:, cut], uref[:, cut], zero], axis=1)

    state = start[...]
    xs[0] = state
    for n in range(slices):
        state = advance(state, n) + packed(by, bu, n)
        xs[n + 1] = state

    lane_of = lax.broadcasted_iota(jnp.int32, (1, LANES), 1)
    scale = jnp.where(lane_of < DOF, TWO_PI, to_u)

    def iteration(k, corrections):
        for n in range(slices):
            cut = pl.ds(plan.where[n], DOF)
            ybuf[:, cut] = xs[n, :, 0:DOF]
            ubuf[:, cut] = xs[n, :, DOF : 2 * DOF]
        for j in range(HS):

            def substep(counter, carry):
                result = []
                for g, (base, width, first, count) in enumerate(plan.groups):
                    y, u = carry[g]
                    cut = pl.ds(base, width)
                    t = y - jnp.round(y)
                    s = t * t
                    poly = jnp.full_like(s, SIN[-1])
                    for c in SIN[-2::-1]:
                        poly = poly * s + c
                    force = (
                        tq[j, :, cut]
                        - spring[j, :, cut] * y
                        - fric[j, :, cut] * u
                        - (grav[:, cut] * t) * poly
                    )
                    u = u + product(force, g, width)
                    y = y + u
                    result.append((y, u))
                return tuple(result)

            first_state = tuple(
                (ybuf[:, pl.ds(base, width)], ubuf[:, pl.ds(base, width)])
                for base, width, first, count in plan.groups
            )
            last = lax.fori_loop(0, SUB, substep, first_state)
            for g, (base, width, first, count) in enumerate(plan.groups):
                ybuf[:, pl.ds(base, width)] = last[g][0]
                ubuf[:, pl.ds(base, width)] = last[g][1]
        worst = jnp.zeros((epd, 1), F32)
        change = None
        for n in range(slices):
            jump = packed(ybuf, ubuf, n) - xs[n + 1]
            change = jump if change is None else advance(change, n) + jump
            real = change * scale
            worst = jnp.maximum(worst, jnp.sum(real * real, axis=1, keepdims=True))
            xs[n + 1] = xs[n + 1] + change
        return jnp.where(lane_of == k, jnp.sqrt(worst), corrections)

    corrections = lax.fori_loop(0, ITERS, iteration, jnp.zeros((epd, LANES), F32))
    rows_of = 2 * DOF
    for n in range(slices):
        dst, pos = divmod(n, local)
        out[dst, :, pos * rows_of : (pos + 1) * rows_of] = (xs[n + 1] * scale)[:, :rows_of]
    for dst in range(slices // local):
        out[dst, :, local * rows_of : local * rows_of + ITERS] = corrections[:, :ITERS]


def body(tm, env, init_state, torque, contact, mass_inverse, stiffness, damping, gravity,
         contact_stiffness, contact_damping):
    local = mass_inverse.shape[0]
    steps = torque.shape[0]
    env_local = init_state.shape[1]
    epd = env_local // tm
    slices = local * tm
    plan = Plan(slices)
    vmem = pl.BlockSpec(memory_space=pltpu.VMEM)
    dma = pltpu.SemaphoreType.DMA

    flat = jnp.concatenate(
        [torque.reshape(steps * DOF, env_local), contact.astype(F32)], axis=0
    ).T
    wide = flat.shape[1]
    tx = flat.reshape(tm, epd, wide)
    m2 = mass_inverse.transpose(1, 0, 2).reshape(DOF, local * DOF)
    row = jnp.pad(jnp.sum(contact.astype(F32), axis=1)[None], ((0, 0), (0, LANES - steps)))
    rx, mall, rows = pl.pallas_call(
        functools.partial(exchange_in, tm, env),
        out_shape=(
            jax.ShapeDtypeStruct(tx.shape, F32),
            jax.ShapeDtypeStruct((tm,) + m2.shape, F32),
            jax.ShapeDtypeStruct((tm, env, 1, LANES), F32),
        ),
        in_specs=[vmem] * 3,
        out_specs=(vmem,) * 3,
        scratch_shapes=[dma((tm,))] * 4 + [dma((tm * env,))] * 2,
        compiler_params=pltpu.CompilerParams(collective_id=0, has_side_effects=True),
        name="exchange_in",
    )(tx, m2, row)

    me_t = lax.axis_index("tm")
    mine = lax.dynamic_slice_in_dim(init_state, me_t * epd, epd, axis=1)
    unit = jnp.concatenate([
        jnp.full((DOF, 1), 1.0 / TWO_PI, F32), jnp.full((DOF, 1), fine_dt / TWO_PI, F32)
    ])
    start = jnp.pad((mine * unit).T, ((0, 0), (0, LANES - 2 * DOF)))
    prm = jnp.stack([stiffness, damping, gravity, contact_stiffness, contact_damping])
    depth = -(-2 * DOF // 8) * 8
    lanes = plan.lanes
    groups = len(plan.groups)
    width_out = local * 2 * DOF + ITERS
    big = pltpu.VMEM((epd, lanes), F32)
    both = pltpu.VMEM((HS, epd, lanes), F32)
    thin = pltpu.VMEM((HS, 1, lanes), F32)
    out = pl.pallas_call(
        functools.partial(compute, slices, local, env_local * env),
        out_shape=jax.ShapeDtypeStruct((tm, epd, width_out), F32),
        in_specs=[vmem] * 5,
        out_specs=vmem,
        scratch_shapes=[
            both, both, both, pltpu.VMEM((1, lanes), F32), thin, thin,
            pltpu.VMEM((groups, WIDE, WIDE), BF16), pltpu.VMEM((groups, WIDE, WIDE), BF16),
            pltpu.VMEM((WIDE, WIDE), F32),
            big, big, big, big,
            pltpu.VMEM((depth, lanes), F32), pltpu.VMEM((depth, lanes), F32),
            pltpu.VMEM((slices, 2 * LANES, 2 * LANES), BF16),
            pltpu.VMEM((LANES, LANES), F32),
            pltpu.VMEM((slices + 1, epd, LANES), F32),
        ],
        name="parareal",
    )(rx, mall, rows, start, prm)

    back = pl.pallas_call(
        functools.partial(exchange_out, tm),
        out_shape=jax.ShapeDtypeStruct(out.shape, F32),
        in_specs=[vmem],
        out_specs=vmem,
        scratch_shapes=[dma((tm,))] * 2,
        compiler_params=pltpu.CompilerParams(collective_id=1, has_side_effects=True),
        name="exchange_out",
    )(out)
    turned = back.reshape(env_local, width_out).T
    states = turned[: local * 2 * DOF].reshape(local, 2 * DOF, env_local)
    return states, turned[local * 2 * DOF :]


def solution(mesh):
    placed = (
        P(None, "env"),
        P("tm", None, "env"),
        P("tm", "env"),
        P("tm", None, None),
        P(),
        P(),
        P(),
        P(),
        P(),
    )
    return jax.shard_map(
        functools.partial(body, mesh.shape["tm"], mesh.shape["env"]),
        mesh=mesh,
        in_specs=placed,
        out_specs=(P("tm", None, "env"), P(None, "env")),
        check_vma=False,
    )
```

time: 318 us -> 104 us (0.33)
  blocking collectives: 187 us -> 0 us
  matrix products: 111 us -> 0 us
  Pallas kernels: 0 us -> 93.8 us
  loops' own time: 7.26 us -> 0 us
    all_gather x5 -> x0, blocking collectives: 157 us -> none  [the longest x4 126 us: sweep(): lax.all_gather(local_shift[None], 'tm', axis=0, tiled=True)]
    dot_general x227 -> x0, matrix products: 111 us -> none  [the longest x220 108 us: exact_dot(): jnp.dot(left, right, precision=lax.Precision.HIGHEST, preferred_element_t...]
    pallas_call x0 -> x3, Pallas kernels: none -> 93.8 us  [the longest x1 63.8 us: body(): pl.pallas_call(functools.partial(compute, slices, local, env_local * env)...]
    pmax x1 -> x0, blocking collectives: 21.2 us -> none  [body(): records.append(lax.pmax(local_max, 'tm'))]
    psum x1 -> x0, blocking collectives: 8.39 us -> none  [body(): totals = lax.psum(jnp.sum(contact_float, axis=1), 'env')]
    another operation x7 -> x0, loops' own time: 7.26 us -> none  [the longest x1 5.4 us: body(): lax.scan(backward, eye_state, (positions, all_maps), reverse=True)]
    dynamic_slice x8 -> x1, local copies, waits for them, and re-layouts: 4.98 us -> 0.08 us  [body(): mine = lax.dynamic_slice_in_dim(init_state, me_t * epd, epd, axis=1)]
where the time goes in v1:
time: 104 us; the launch traced here: 103 us
  Pallas kernels  93.8 us (90%)
  local copies, waits for them, and re-layouts  8.06 us (8%)
    pallas_call x1, Pallas kernels, body(): pl.pallas_call(functools.partial(compute, slices, local, env_local * env)...  63.8 us
    pallas_call x1, Pallas kernels, body(): pl.pallas_call(functools.partial(exchange_in, tm, env), out_shape=(jax.Sh...  17.4 us
    pallas_call x1, Pallas kernels, body(): pl.pallas_call(functools.partial(exchange_out, tm), out_shape=jax.ShapeDt...  12.7 us
    unnamed x21, local copies, waits for them, and re-layouts  3.03 us

profile of v1, /device:TPU:0, one launch (start us, length us, event | category | flops | bytes accessed | tf_op | source)
XLA Modules:
  0.0 103.5 jit_solution(10873782537163352521)
XLA Ops:
  0.6 0.0 copy-start
  0.6 0.7 convert_element_type.8
  1.4 0.9 copy.14
  2.4 0.0 copy-start.1
  2.4 0.8 copy.15
  3.2 0.0 copy-done.1
  3.2 0.0 copy-start.2
  3.2 0.7 reshape.21.m2
  3.9 0.0 copy-done.2
  3.9 0.1 convert_reduce_fusion
  4.0 0.5 pad.8.row
  4.5 17.4 %exchange_in.1 = (f32[8,32,144]{2,1,0:T(8,128)}, f32[8,35,70]{2,1,0:T(8,128)}, f32[8,4,1,128]{3,2,1,0:T(1,128)}) custom-call(f32[8,32,144]{2,1,0:T(8,128)} %bitcast.15, f32[35,70]{1,0:T(8,128)} %reshape.21.m2, f32[1,128]{1,0:T(1,128)} %pad.8.row), custom_call_target="tpu_custom_call" | custom-call | tf_op jit(solution)/shard_map/exchange_in/pallas_call | solution.py:346
  21.9 0.0 copy-done
  21.9 0.1 constant_dynamic-slice_fusion
  22.0 0.0 copy-start.3
  22.0 0.1 copy.19
  22.1 0.6 copy-done.3
  22.7 0.0 copy-start.7
  22.7 0.0 copy-start.8
  22.7 0.6 pad.9.start
  23.3 0.0 copy-start.4
  23.3 0.0 copy-start.5
  23.3 0.0 copy-start.6
  23.3 0.0 copy-done.7
  23.4 0.0 copy-done.8
  23.4 0.6 copy-done.4
  24.0 0.0 copy-done.5
  24.0 0.0 copy-done.6
  24.0 0.6 stack.23.prm
  24.6 63.8 %parareal.1.tx = f32[8,32,143]{2,1,0:T(8,128)} custom-call(f32[8,32,144]{2,1,0:T(8,128)} %get-tuple-element.5.rx, f32[8,35,70]{2,1,0:T(8,128)} %get-tuple-element.6.mall, f32[8,4,1,128]{3,2,1,0:T(1,128)} %get-tuple-element.7.rows, f32[32,128]{1,0:T(8,128)} %pad.9.start, f32[5,35]{1,0:T(8,128)} %stack.23.prm), custom_call_target="tpu_custom_call" | custom-call | tf_op jit(solution)/shard_map/parareal/pallas_call | solution.py:374
  88.4 12.7 %exchange_out.1 = f32[8,32,143]{2,1,0:T(8,128)} custom-call(f32[8,32,143]{2,1,0:T(8,128)} %parareal.1.tx), custom_call_target="tpu_custom_call" | custom-call | tf_op jit(solution)/shard_map/exchange_out/pallas_call | solution.py:392
  101.1 1.0 %copy.17 = f32[256,143]{0,1:T(8,128)S(1)} copy(f32[256,143]{1,0:T(8,128)} %bitcast.16) | data formatting | bytes 292864 | tf_op jit(solution)/shard_map/reshape | solution.py:401
  102.2 0.7 copy.18
  102.9 0.6 slice.9
  (4 shorter events, 0.1 us)
Async XLA Ops:
  0.6 21.3 %copy-start = (f32[70,256]{1,0:T(8,128)S(1)}, f32[70,256]{1,0:T(8,128)}, u32[]{:S(2)}) copy-start(f32[70,256]{1,0:T(8,128)} %param.9) | copy-start | bytes 215044
  2.4 0.8 copy-start.1
  3.2 0.7 copy-start.2
  22.0 0.7 copy-start.3
  22.7 0.7 copy-start.7
  22.7 0.7 copy-start.8
  23.3 0.7 copy-start.4
  23.3 0.7 copy-start.5
  23.3 0.7 copy-start.6

commit v2 on v1

--- a/solution.py
+++ b/solution.py
@@ -148,7 +148,7 @@
 
 class Plan:
     def __init__(self, slices):
-        per = WIDE // DOF
+        per = LANES // DOF
         self.groups = []
         self.where = []
         base = 0
@@ -164,18 +164,15 @@
 
 def compute(
     slices, local, total_env,
-    rx, mall, rows, start, prm,
+    rx, mall, rows, stiff, damp, gravity, cstiff, cdamp,
     out,
-    tq, spring, fric, grav, cspring, cfric, whi, wlo, wtmp, ybuf, ubuf, by, bu, ly, lu, cmap, ctmp, xs,
+    tq, spring, fric, grav, cspring, cfric, wgt, wtmp, ybuf, ubuf, by, bu, ly, lu, cmap, ctmp, xs,
 ):
     plan = Plan(slices)
-    epd = start.shape[0]
+    epd = rx.shape[1]
     ratio = float(SUB)
-    stiff = prm[0:1, :]
-    damp = prm[1:2, :]
-    gravity = prm[2:3, :]
-    cstiff = prm[3:4, :]
-    cdamp = prm[4:5, :]
+    unroll = max(1, min(SUB, 48 // len(plan.groups)))
+    stiff, damp, gravity, cstiff, cdamp = (r[...] for r in (stiff, damp, gravity, cstiff, cdamp))
     to_u = TWO_PI / fine_dt
 
     for ref in (tq, spring, fric, grav, cspring, cfric, ybuf, ubuf, ly, lu):
@@ -208,14 +205,15 @@
                 fine_dt * fine_dt / TWO_PI
             ) * mall[src, :, here * DOF : (here + 1) * DOF]
         high, low = split(wtmp[...])
-        whi[g] = high
-        wlo[g] = low
+        wgt[g, 0:LANES, 0:LANES] = high
+        wgt[g, LANES:, 0:LANES] = high
+        wgt[g, 0:LANES, LANES:] = low
+        wgt[g, LANES:, LANES:] = jnp.zeros_like(low)
 
     def product(force, g, width):
         high, low = split(force)
-        upper = whi[g, :width, :width]
-        lower = wlo[g, :width, :width]
-        return dot(high, upper) + dot(low, upper) + dot(high, lower)
+        both = dot(jnp.concatenate([high, low], axis=1), wgt[g])
+        return both[:, :LANES] + both[:, LANES:]
 
     rank = lax.broadcasted_iota(jnp.int32, (ly.shape[0], DOF), 0)
     col = lax.broadcasted_iota(jnp.int32, (ly.shape[0], DOF), 1)
@@ -261,14 +259,16 @@
         zero = jnp.zeros((epd, LANES - 2 * DOF), F32)
         return jnp.concatenate([yref[:, cut], uref[:, cut], zero], axis=1)
 
-    state = start[...]
+    lane_of = lax.broadcasted_iota(jnp.int32, (1, LANES), 1)
+    scale = jnp.where(lane_of < DOF, TWO_PI, to_u)
+    shrink = jnp.where(lane_of < DOF, 1.0 / TWO_PI, 1.0 / to_u)
+    first_lane = local * HS * (DOF + 1)
+    own = rx[lax.axis_index("tm")][:, first_lane : first_lane + 2 * DOF]
+    state = jnp.concatenate([own, jnp.zeros((epd, LANES - 2 * DOF), F32)], axis=1) * shrink
     xs[0] = state
     for n in range(slices):
         state = advance(state, n) + packed(by, bu, n)
         xs[n + 1] = state
-
-    lane_of = lax.broadcasted_iota(jnp.int32, (1, LANES), 1)
-    scale = jnp.where(lane_of < DOF, TWO_PI, to_u)
 
     def iteration(k, corrections):
         for n in range(slices):
@@ -302,7 +302,7 @@
                 (ybuf[:, pl.ds(base, width)], ubuf[:, pl.ds(base, width)])
                 for base, width, first, count in plan.groups
             )
-            last = lax.fori_loop(0, SUB, substep, first_state)
+            last = lax.fori_loop(0, SUB, substep, first_state, unroll=unroll)
             for g, (base, width, first, count) in enumerate(plan.groups):
                 ybuf[:, pl.ds(base, width)] = last[g][0]
                 ubuf[:, pl.ds(base, width)] = last[g][1]
@@ -337,7 +337,7 @@
     dma = pltpu.SemaphoreType.DMA
 
     flat = jnp.concatenate(
-        [torque.reshape(steps * DOF, env_local), contact.astype(F32)], axis=0
+        [torque.reshape(steps * DOF, env_local), contact.astype(F32), init_state], axis=0
     ).T
     wide = flat.shape[1]
     tx = flat.reshape(tm, epd, wide)
@@ -357,13 +357,7 @@
         name="exchange_in",
     )(tx, m2, row)
 
-    me_t = lax.axis_index("tm")
-    mine = lax.dynamic_slice_in_dim(init_state, me_t * epd, epd, axis=1)
-    unit = jnp.concatenate([
-        jnp.full((DOF, 1), 1.0 / TWO_PI, F32), jnp.full((DOF, 1), fine_dt / TWO_PI, F32)
-    ])
-    start = jnp.pad((mine * unit).T, ((0, 0), (0, LANES - 2 * DOF)))
-    prm = jnp.stack([stiffness, damping, gravity, contact_stiffness, contact_damping])
+    prm = [p.reshape(1, DOF) for p in (stiffness, damping, gravity, contact_stiffness, contact_damping)]
     depth = -(-2 * DOF // 8) * 8
     lanes = plan.lanes
     groups = len(plan.groups)
@@ -374,12 +368,12 @@
     out = pl.pallas_call(
         functools.partial(compute, slices, local, env_local * env),
         out_shape=jax.ShapeDtypeStruct((tm, epd, width_out), F32),
-        in_specs=[vmem] * 5,
+        in_specs=[vmem] * 8,
         out_specs=vmem,
         scratch_shapes=[
             both, both, both, pltpu.VMEM((1, lanes), F32), thin, thin,
-            pltpu.VMEM((groups, WIDE, WIDE), BF16), pltpu.VMEM((groups, WIDE, WIDE), BF16),
-            pltpu.VMEM((WIDE, WIDE), F32),
+            pltpu.VMEM((groups, WIDE, WIDE), BF16),
+            pltpu.VMEM((LANES, LANES), F32),
             big, big, big, big,
             pltpu.VMEM((depth, lanes), F32), pltpu.VMEM((depth, lanes), F32),
             pltpu.VMEM((slices, 2 * LANES, 2 * LANES), BF16),
@@ -387,7 +381,7 @@
             pltpu.VMEM((slices + 1, epd, LANES), F32),
         ],
         name="parareal",
-    )(rx, mall, rows, start, prm)
+    )(rx, mall, rows, *prm)
 
     back = pl.pallas_call(
         functools.partial(exchange_out, tm),

time: 104 us -> 80.7 us (0.78)
  Pallas kernels: 93.8 us -> 71.8 us
    pallas_call x1, Pallas kernels: 63.8 us -> 41.7 us  [body(): pl.pallas_call(functools.partial(compute, slices, local, env_local * env)...]
    unnamed x21 -> x6, local copies, waits for them, and re-layouts: 3.03 us -> 3.2 us
where the time goes in v2:
time: 80.7 us; the launch traced here: 80.3 us
  Pallas kernels  71.8 us (89%)
  local copies, waits for them, and re-layouts  7.69 us (10%)
    pallas_call x1, Pallas kernels, body(): pl.pallas_call(functools.partial(compute, slices, local, env_local * env)...  41.7 us
    pallas_call x1, Pallas kernels, body(): pl.pallas_call(functools.partial(exchange_in, tm, env), out_shape=(jax.Sh...  17.4 us
    pallas_call x1, Pallas kernels, body(): pl.pallas_call(functools.partial(exchange_out, tm), out_shape=jax.ShapeDt...  12.7 us
    unnamed x6, local copies, waits for them, and re-layouts  3.2 us

profile of v2, /device:TPU:0, one launch (start us, length us, event | category | flops | bytes accessed | tf_op | source)
XLA Modules:
  0.0 80.3 jit_solution(13403311070479374059)
XLA Ops:
  0.6 0.0 copy-start.1
  0.6 0.7 copy-done.1
  1.3 0.1 convert_reduce_fusion
  1.4 0.5 pad.4.row
  2.0 1.5 %reshape.36.m2 = f32[35,70]{1,0:T(8,128)} reshape(f32[35,2,35]{2,1,0:T(2,128)} %bitcast.17) | data formatting | bytes 19600 | tf_op jit(solution)/shard_map/reshape | solution.py:344
  3.4 0.9 %copy.14 = f32[4,35,256]{2,1,0:T(8,128)S(1)} copy(f32[4,35,256]{2,0,1:T(4,128)} %param.10) | data formatting | bytes 286720 | tf_op args[1]
  4.4 0.0 copy-start
  4.4 0.8 %copy-done = f32[70,256]{1,0:T(8,128)S(1)} copy-done((f32[70,256]{1,0:T(8,128)S(1)}, f32[70,256]{1,0:T(8,128)}, u32[]{:S(2)}) %copy-start) | copy-done | bytes 71704
  5.3 0.8 %copy.15 = f32[256,214]{1,0:T(8,128)} copy(f32[256,214]{0,1:T(8,128)S(1)} %maximum_bitcast_fusion) | data formatting | bytes 438272 | tf_op jit(solution)/shard_map/transpose | solution.py:341
  6.1 17.4 %exchange_in.1 = (f32[8,32,214]{2,1,0:T(8,128)}, f32[8,35,70]{2,1,0:T(8,128)}, f32[8,4,1,128]{3,2,1,0:T(1,128)}) custom-call(f32[8,32,214]{2,1,0:T(8,128)} %bitcast.14, f32[35,70]{1,0:T(8,128)} %reshape.36.m2, f32[1,128]{1,0:T(1,128)} %pad.4.row), custom_call_target="tpu_custom_call" | custom-call | tf_op jit(solution)/shard_map/exchange_in/pallas_call | solution.py:346
  23.5 41.7 %parareal.1.tx = f32[8,32,143]{2,1,0:T(8,128)} custom-call(f32[8,32,214]{2,1,0:T(8,128)} %get-tuple-element.5.rx, f32[8,35,70]{2,1,0:T(8,128)} %get-tuple-element.6.mall, f32[8,4,1,128]{3,2,1,0:T(1,128)} %get-tuple-element.7.rows, f32[1,35]{1,0:T(1,128)} %bitcast.18, f32[1,35]{1,0:T(1,128)} %bitcast.19, f32[1,35]{1,0:T(1,128)} %bitcast.20, ...), custom_call_target="tpu_custom_call" | custom-call | tf_op jit(solution)/shard_map/parareal/pallas_call | solution.py:368
  65.2 12.7 %exchange_out.1 = f32[8,32,143]{2,1,0:T(8,128)} custom-call(f32[8,32,143]{2,1,0:T(8,128)} %parareal.1.tx), custom_call_target="tpu_custom_call" | custom-call | tf_op jit(solution)/shard_map/exchange_out/pallas_call | solution.py:386
  77.9 1.0 %copy.16 = f32[256,143]{0,1:T(8,128)S(1)} copy(f32[256,143]{1,0:T(8,128)} %bitcast.13) | data formatting | bytes 292864 | tf_op jit(solution)/shard_map/reshape | solution.py:395
  79.0 0.6 slice.9
  79.6 0.7 copy.17
  (4 shorter events, 0.1 us)
Async XLA Ops:
  0.6 0.7 copy-start.1
  4.4 0.9 %copy-start = (f32[70,256]{1,0:T(8,128)S(1)}, f32[70,256]{1,0:T(8,128)}, u32[]{:S(2)}) copy-start(f32[70,256]{1,0:T(8,128)} %param.9) | copy-start | bytes 215044

commit v3 on v2

--- a/solution.py
+++ b/solution.py
@@ -166,12 +166,13 @@
     slices, local, total_env,
     rx, mall, rows, stiff, damp, gravity, cstiff, cdamp,
     out,
-    tq, spring, fric, grav, cspring, cfric, wgt, wtmp, ybuf, ubuf, by, bu, ly, lu, cmap, ctmp, xs,
+    tq, spring, fric, grav, cspring, cfric, wgt, wtmp, ybuf, ubuf, by, bu, ly, lu, cmap, pmap, ctmp, xs,
 ):
     plan = Plan(slices)
     epd = rx.shape[1]
     ratio = float(SUB)
-    unroll = max(1, min(SUB, 48 // len(plan.groups)))
+    block = 4 if slices % 4 == 0 else 1
+    unroll = max(1, min(SUB, 96 // len(plan.groups)))
     stiff, damp, gravity, cstiff, cdamp = (r[...] for r in (stiff, damp, gravity, cstiff, cdamp))
     to_u = TWO_PI / fine_dt
 
@@ -249,10 +250,44 @@
         cmap[n, LANES:, 0:LANES] = high
         cmap[n, 0:LANES, LANES:] = low
 
-    def advance(state, n):
+    def through(state, weight):
         high, low = split(state)
-        both = dot(jnp.concatenate([high, low], axis=1), cmap[n])
+        both = dot(jnp.concatenate([high, low], axis=1), weight)
         return both[:, :LANES] + both[:, LANES:]
+
+    firsts = range(0, slices, block)
+    running = {m: jnp.concatenate(
+        [ly[:, pl.ds(plan.where[m], DOF)], lu[:, pl.ds(plan.where[m], DOF)],
+         jnp.zeros((depth, LANES - 2 * DOF), F32)], axis=1) for m in firsts}
+    for i in range(1, block):
+        for m in firsts:
+            running[m] = through(running[m], cmap[m + i])
+            ctmp[0:depth, :] = running[m]
+            high, low = split(ctmp[...])
+            pmap[m + i, 0:LANES, 0:LANES] = high
+            pmap[m + i, LANES:, 0:LANES] = high
+            pmap[m + i, 0:LANES, LANES:] = low
+            pmap[m + i, LANES:, LANES:] = jnp.zeros_like(low)
+
+    def sweep(offsets, entry):
+        ends = list(offsets)
+        for i in range(1, block):
+            for m in firsts:
+                ends[m + i] = through(ends[m + i - 1], cmap[m + i]) + ends[m + i]
+        enter = {}
+        for m in firsts:
+            enter[m] = entry
+            last = m + block - 1
+            whole = pmap if block > 1 else cmap
+            if entry is not None:
+                ends[last] = ends[last] + through(entry, whole[last])
+            entry = ends[last]
+        for i in range(block - 1):
+            for m in firsts:
+                if enter[m] is not None:
+                    part = cmap if i == 0 else pmap
+                    ends[m + i] = ends[m + i] + through(enter[m], part[m + i])
+        return ends
 
     def packed(yref, uref, n):
         cut = pl.ds(plan.where[n], DOF)
@@ -266,9 +301,9 @@
     own = rx[lax.axis_index("tm")][:, first_lane : first_lane + 2 * DOF]
     state = jnp.concatenate([own, jnp.zeros((epd, LANES - 2 * DOF), F32)], axis=1) * shrink
     xs[0] = state
+    ends = sweep([packed(by, bu, n) for n in range(slices)], state)
     for n in range(slices):
-        state = advance(state, n) + packed(by, bu, n)
-        xs[n + 1] = state
+        xs[n + 1] = ends[n]
 
     def iteration(k, corrections):
         for n in range(slices):
@@ -307,13 +342,11 @@
                 ybuf[:, pl.ds(base, width)] = last[g][0]
                 ubuf[:, pl.ds(base, width)] = last[g][1]
         worst = jnp.zeros((epd, 1), F32)
-        change = None
+        changes = sweep([packed(ybuf, ubuf, n) - xs[n + 1] for n in range(slices)], None)
         for n in range(slices):
-            jump = packed(ybuf, ubuf, n) - xs[n + 1]
-            change = jump if change is None else advance(change, n) + jump
-            real = change * scale
+            real = changes[n] * scale
             worst = jnp.maximum(worst, jnp.sum(real * real, axis=1, keepdims=True))
-            xs[n + 1] = xs[n + 1] + change
+            xs[n + 1] = xs[n + 1] + changes[n]
         return jnp.where(lane_of == k, jnp.sqrt(worst), corrections)
 
     corrections = lax.fori_loop(0, ITERS, iteration, jnp.zeros((epd, LANES), F32))
@@ -377,6 +410,7 @@
             big, big, big, big,
             pltpu.VMEM((depth, lanes), F32), pltpu.VMEM((depth, lanes), F32),
             pltpu.VMEM((slices, 2 * LANES, 2 * LANES), BF16),
+            pltpu.VMEM((slices, 2 * LANES, 2 * LANES), BF16),
             pltpu.VMEM((LANES, LANES), F32),
             pltpu.VMEM((slices + 1, epd, LANES), F32),
         ],

time: 80.7 us -> 76.2 us (0.944)
  Pallas kernels: 71.8 us -> 67.3 us
    pallas_call x1, Pallas kernels: 41.7 us -> 37.2 us  [body(): pl.pallas_call(functools.partial(compute, slices, local, env_local * env)...]
where the time goes in v3:
time: 76.2 us; the launch traced here: 75.9 us
  Pallas kernels  67.3 us (88%)
  local copies, waits for them, and re-layouts  7.69 us (10%)
    pallas_call x1, Pallas kernels, body(): pl.pallas_call(functools.partial(compute, slices, local, env_local * env)...  37.2 us
    pallas_call x1, Pallas kernels, body(): pl.pallas_call(functools.partial(exchange_in, tm, env), out_shape=(jax.Sh...  17.4 us
    pallas_call x1, Pallas kernels, body(): pl.pallas_call(functools.partial(exchange_out, tm), out_shape=jax.ShapeDt...  12.7 us
    unnamed x6, local copies, waits for them, and re-layouts  3.2 us

profile of v3, /device:TPU:0, one launch (start us, length us, event | category | flops | bytes accessed | tf_op | source)
XLA Modules:
  0.0 75.9 jit_solution(16470762958396341117)
XLA Ops:
  0.6 0.0 copy-start.1
  0.6 0.7 copy-done.1
  1.3 0.1 convert_reduce_fusion
  1.4 0.5 pad.4.row
  2.0 1.5 %reshape.36.m2 = f32[35,70]{1,0:T(8,128)} reshape(f32[35,2,35]{2,1,0:T(2,128)} %bitcast.17) | data formatting | bytes 19600 | tf_op jit(solution)/shard_map/reshape | solution.py:377
  3.4 0.9 %copy.14 = f32[4,35,256]{2,1,0:T(8,128)S(1)} copy(f32[4,35,256]{2,0,1:T(4,128)} %param.10) | data formatting | bytes 286720 | tf_op args[1]
  4.4 0.0 copy-start
  4.4 0.8 %copy-done = f32[70,256]{1,0:T(8,128)S(1)} copy-done((f32[70,256]{1,0:T(8,128)S(1)}, f32[70,256]{1,0:T(8,128)}, u32[]{:S(2)}) %copy-start) | copy-done | bytes 71704
  5.3 0.8 %copy.15 = f32[256,214]{1,0:T(8,128)} copy(f32[256,214]{0,1:T(8,128)S(1)} %maximum_bitcast_fusion) | data formatting | bytes 438272 | tf_op jit(solution)/shard_map/transpose | solution.py:374
  6.1 17.4 %exchange_in.1 = (f32[8,32,214]{2,1,0:T(8,128)}, f32[8,35,70]{2,1,0:T(8,128)}, f32[8,4,1,128]{3,2,1,0:T(1,128)}) custom-call(f32[8,32,214]{2,1,0:T(8,128)} %bitcast.14, f32[35,70]{1,0:T(8,128)} %reshape.36.m2, f32[1,128]{1,0:T(1,128)} %pad.4.row), custom_call_target="tpu_custom_call" | custom-call | tf_op jit(solution)/shard_map/exchange_in/pallas_call | solution.py:379
  23.5 37.2 %parareal.1.tx = f32[8,32,143]{2,1,0:T(8,128)} custom-call(f32[8,32,214]{2,1,0:T(8,128)} %get-tuple-element.5.rx, f32[8,35,70]{2,1,0:T(8,128)} %get-tuple-element.6.mall, f32[8,4,1,128]{3,2,1,0:T(1,128)} %get-tuple-element.7.rows, f32[1,35]{1,0:T(1,128)} %bitcast.18, f32[1,35]{1,0:T(1,128)} %bitcast.19, f32[1,35]{1,0:T(1,128)} %bitcast.20, ...), custom_call_target="tpu_custom_call" | custom-call | tf_op jit(solution)/shard_map/parareal/pallas_call | solution.py:401
  60.7 12.7 %exchange_out.1 = f32[8,32,143]{2,1,0:T(8,128)} custom-call(f32[8,32,143]{2,1,0:T(8,128)} %parareal.1.tx), custom_call_target="tpu_custom_call" | custom-call | tf_op jit(solution)/shard_map/exchange_out/pallas_call | solution.py:420
  73.5 1.0 %copy.16 = f32[256,143]{0,1:T(8,128)S(1)} copy(f32[256,143]{1,0:T(8,128)} %bitcast.13) | data formatting | bytes 292864 | tf_op jit(solution)/shard_map/reshape | solution.py:429
  74.5 0.6 slice.9
  75.1 0.7 copy.17
  (4 shorter events, 0.1 us)
Async XLA Ops:
  0.6 0.7 copy-start.1
  4.4 0.9 %copy-start = (f32[70,256]{1,0:T(8,128)S(1)}, f32[70,256]{1,0:T(8,128)}, u32[]{:S(2)}) copy-start(f32[70,256]{1,0:T(8,128)} %param.9) | copy-start | bytes 215044
